TPU v7x, 32 devices: a whole 2x2x4 slice. The times are simulated.
32 devices in a mesh: elem: 8 (over z, y), comp: 2 (over x), rep: 2 (over core).
Axes of the slice: x: 2, y: 2, z: 4, core: 2. Of those that a mesh axis runs over, the one named last changes fastest.
Arguments:
- velocity: float32 [3, 10, 10, 10, 2, 6144], P(None, 'comp', None, None, None, ('elem', 'rep')), may hold values from -6 to 6
- geometry: float32 [3, 3, 10, 10, 10, 2, 6144], P(None, None, 'comp', None, None, None, ('elem', 'rep')), may hold values from -40 to 40
- element_place: int32 [2, 6144], P('comp', ('elem', 'rep')), may hold values from 0 to 383, as said below
Outputs:
- pressure: float32 [10, 10, 10, 2, 6144], P(None, None, None, 'comp', ('elem', 'rep'))
Inputs may be any that keep to these rules, and one draw needn't show every extreme that they name: `element_place`: in each row and each aligned run of 384 entries of it, every value 0 to 383 appears once.
All inputs are finite; a program needn't handle non-finite values.
Results may differ from a plain program's by a relative error of at most 0.000071.
Values sent between devices are 32-bit elements; how exact they have to be, the bound alone decides.
No kernel may reach another device: no remote copies, remote signals or barrier semaphores. Data moves between devices by JAX's collectives and lax.ppermute only.
A program may use at most 192 MiB of HBM per device.

v0:
```python
import jax
import jax.numpy as jnp
import numpy as np
from jax import lax
from jax.sharding import PartitionSpec as P

BLOCK_X = 6
BLOCK_Y = 8
BLOCK_Z = 8
GRID_Y = 4
exact_mode = lax.Precision.HIGHEST


def passed_along(x, axis, by):
    count = lax.axis_size(axis)
    pairs = [(i, i + by) for i in range(count) if 0 <= i + by < count]
    return lax.ppermute(x, axis, pairs)


def legendre_columns(points, degree):
    columns = [points * 0.0 + 1.0, points]
    for order in range(2, degree + 1):
        columns.append(
            ((2 * order - 1) * points * columns[order - 1] - (order - 1) * columns[order - 2])
            / order
        )
    return columns


def derivative_table(node_count):
    degree = node_count - 1
    points = np.cos(np.pi * np.arange(node_count) / degree)
    for sweep in range(100):
        columns = legendre_columns(points, degree)
        points = points - (points * columns[degree] - columns[degree - 1]) / (
            node_count * columns[degree]
        )
    points = np.sort(points)
    values = legendre_columns(points, degree)[degree]
    identity = np.eye(node_count)
    spacing = points[:, None] - points[None, :] + identity
    matrix = values[:, None] / (values[None, :] * spacing)
    matrix = np.where(identity > 0.5, 0.0, matrix)
    matrix[0, 0] = -degree * (degree + 1) / 4.0
    matrix[degree, degree] = degree * (degree + 1) / 4.0
    return matrix


def apply_transpose(deriv_table, flux_r, flux_s, flux_t):
    along_r = jnp.einsum("ia,i...->a...", deriv_table, flux_r, precision=exact_mode)
    along_s = jnp.einsum("ib,ai...->ab...", deriv_table, flux_s, precision=exact_mode)
    along_t = jnp.einsum("ic,abi...->abc...", deriv_table, flux_t, precision=exact_mode)
    return along_r + along_s + along_t


def local_pass(field, direction, block_grid):
    last_node = field.shape[0] - 1
    element_axis = 3 + direction
    extent = block_grid[direction]
    lower = lax.slice_in_dim(field, 0, 1, axis=direction)
    upper = lax.slice_in_dim(field, last_node, last_node + 1, axis=direction)
    zero_lower = jnp.zeros_like(lax.slice_in_dim(lower, 0, 1, axis=element_axis))
    add_upper = jnp.concatenate(
        [lax.slice_in_dim(lower, 1, extent, axis=element_axis), zero_lower], axis=element_axis
    )
    add_lower = jnp.concatenate(
        [zero_lower, lax.slice_in_dim(upper, 0, extent - 1, axis=element_axis)], axis=element_axis
    )
    node_iota = lax.broadcasted_iota(jnp.int32, field.shape, direction)
    field = field + jnp.where(node_iota == 0, add_lower, 0.0)
    return field + jnp.where(node_iota == last_node, add_upper, 0.0)


def node_keep(sign_code, last_node):
    if sign_code > 0:
        return slice(last_node, last_node + 1)
    if sign_code < 0:
        return slice(0, 1)
    return slice(None)


def element_keep(sign_code, extent):
    if sign_code > 0:
        return slice(extent - 1, extent)
    if sign_code < 0:
        return slice(0, 1)
    return slice(None)


def take_region(field, offset, block_grid):
    last_node = field.shape[0] - 1
    nodes_key = tuple((node_keep(component, last_node) for component in offset))
    elems_key = tuple(
        (element_keep(offset[dim_index], block_grid[dim_index]) for dim_index in range(3))
    )
    return field[nodes_key + elems_key]


def region_mask(shape, offset, block_grid):
    last_node = shape[0] - 1
    verdict = jnp.ones(shape, dtype=jnp.bool_)
    for dim_index in range(3):
        if offset[dim_index] != 0:
            node_target = last_node if offset[dim_index] > 0 else 0
            elem_target = block_grid[dim_index] - 1 if offset[dim_index] > 0 else 0
            verdict = jnp.logical_and(
                verdict, lax.broadcasted_iota(jnp.int32, shape, dim_index) == node_target
            )
            verdict = jnp.logical_and(
                verdict, lax.broadcasted_iota(jnp.int32, shape, 3 + dim_index) == elem_target
            )
    return verdict


def add_region(field, offset, values, block_grid):
    return field + jnp.where(region_mask(field.shape, offset, block_grid), values, 0.0)


def neighbor_offsets():
    listing = []
    for step_x in (-1, 0, 1):
        for step_y in (-1, 0, 1):
            for step_z in (-1, 0, 1):
                if step_x != 0 or step_y != 0 or step_z != 0:
                    listing.append((step_x, step_y, step_z))
    return listing


def inside(position, offset, extents):
    verdict = jnp.asarray(True)
    for dim_index in range(3):
        target = position[dim_index] + offset[dim_index]
        verdict = jnp.logical_and(
            verdict, jnp.logical_and(target >= 0, target < extents[dim_index])
        )
    return verdict


def body(velocity, geometry, element_place):
    comp_count = lax.axis_size("comp")
    half_nodes = velocity.shape[1]
    node_count = half_nodes * comp_count
    deriv_table = jnp.asarray(derivative_table(node_count), jnp.float32)
    fluxes = []
    for direction in range(3):
        fluxes.append(
            geometry[0, direction] * velocity[0]
            + geometry[1, direction] * velocity[1]
            + geometry[2, direction] * velocity[2]
        )
    flux_r, flux_s, flux_t = (
        lax.all_to_all(fluxes[0], "comp", split_axis=3, concat_axis=0, tiled=True),
        lax.all_to_all(fluxes[1], "comp", split_axis=3, concat_axis=0, tiled=True),
        lax.all_to_all(fluxes[2], "comp", split_axis=3, concat_axis=0, tiled=True),
    )
    owned_nodes = apply_transpose(deriv_table, flux_r, flux_s, flux_t)
    owned_nodes = owned_nodes[:, :, :, 0, :]
    places = element_place[0]
    sub_count = places.shape[0]
    place_matrix = (places[:, None] == jnp.arange(sub_count, dtype=jnp.int32)[None, :]).astype(
        jnp.float32
    )
    canonical = jnp.einsum("abci,ij->abcj", owned_nodes, place_matrix, precision=exact_mode)
    block_grid = (BLOCK_X, BLOCK_Y, BLOCK_Z)
    canonical = canonical.reshape((node_count, node_count, node_count) + block_grid)
    layers = comp_count * lax.axis_size("rep")
    stride_x = GRID_Y * layers
    strides = (stride_x, layers, 1)
    extents = (lax.axis_size(("elem", "comp", "rep")) // stride_x, GRID_Y, layers)
    device = lax.axis_index(("elem", "comp", "rep"))
    position = (device // stride_x, device // layers % GRID_Y, device % layers)
    local_only = canonical
    for direction in range(3):
        local_only = local_pass(local_only, direction, block_grid)
    assembled = local_only
    for offset in neighbor_offsets():
        opposite = tuple((-component for component in offset))
        outgoing = take_region(local_only, opposite, block_grid)
        shift_by = -sum((component * stride for component, stride in zip(offset, strides)))
        incoming = passed_along(outgoing.reshape(-1), ("elem", "comp", "rep"), shift_by)
        within = inside(position, offset, extents)
        payload = jnp.where(within, incoming, 0.0).reshape(outgoing.shape)
        assembled = add_region(assembled, offset, payload, block_grid)
    assembled = assembled.reshape(node_count, node_count, node_count, sub_count)
    result = jnp.einsum("abcj,ij->abci", assembled, place_matrix, precision=exact_mode)
    return result[:, :, :, None, :]


def solution(mesh):
    placed = (
        P(None, "comp", None, None, None, ("elem", "rep")),
        P(None, None, "comp", None, None, None, ("elem", "rep")),
        P("comp", ("elem", "rep")),
    )
    return jax.shard_map(
        body,
        mesh=mesh,
        in_specs=placed,
        out_specs=P(None, None, None, "comp", ("elem", "rep")),
        check_vma=False,
    )
```

profile of v0, /device:TPU:7, one launch (start us, length us, event | category | flops | bytes accessed | tf_op | source)
XLA Modules:
  0.0 409.7 jit_solution(2351560866955214997)
XLA Ops:
  0.0 3.9 fusion.122
  3.9 7.8 %fusion.121 = (f32[1,1,5,10,10,2,384]{6,5,4,3,2,1,0:T(2,128)S(1)}, f32[1,1,5,10,10,2,384]{6,5,4,3,2,1,0:T(2,128)S(1)}, f32[1,1,5,10,10,2,384]{6,5,4,3,2,1,0:T(2,...) fusion(f32[3,3,5,10,10,2,384]{6,5,4,3,2,1,0:T(2,128)} %param.5), kind=kLoop, calls=%fused_computation.193 | loop fusion | bytes 27648000 | tf_op jit(solution)/shard_map/slice | solution.py:147
  11.7 4.5 %fusion.33 = (f32[5,10,10,2,384]{4,2,1,0,3:T(8,128)}, f32[5,10,10,2,384]{4,2,1,0,3:T(8,128)S(1)}, f32[5,10,10,2,384]{4,2,1,0,3:T(8,128)}) fusion(f32[1,5,10,10,2,384]{5,4,3,2,1,0:T(2,128)S(1)} %get-tuple-element.49, f32[1,1,5,10,10,2,384]{6,5,4,3,2,1,0:T(2,128)S(1)} %get-tuple-element.41, f32[1,5,10,10,2,384]{5,4,3,2,1,0:T(2,128)S(1)} %get-tuple-element.48, ...), kind=kLoop, calls=%fused_computation.61 | loop fusion | flops 5760000 | bytes 23040000 | tf_op jit(solution)/shard_map/add | solution.py:147
  16.2 30.7 %all_to_all.45 = f32[5,10,10,2,384]{4,2,1,0,3:T(8,128)} all-to-all(f32[5,10,10,2,384]{4,2,1,0,3:T(8,128)S(1)} %get-tuple-element.45), channel_id=1, replica_groups=mesh['elem'=8,'comp'=2,'rep'=2] {'comp'}, dimensions={3} | all-to-all | bytes 3072000 | tf_op jit(solution)/shard_map/all_to_all | solution.py:153
  46.9 5.1 %all-to-all-start.2 = ((f32[5,10,10,2,384]{4,2,1,0,3:T(8,128)}), f32[5,10,10,2,384]{4,2,1,0,3:T(8,128)S(1)}, u32[]{:S(2)}, u32[]{:S(2)}) async-start(f32[5,10,10,2,384]{4,2,1,0,3:T(8,128)} %get-tuple-element.46), calls=%async_computation.2 | async-start | bytes 4915200 | tf_op jit(solution)/shard_map/all_to_all | solution.py:154
  56.3 21.8 %all-to-all-done.2 = f32[5,10,10,2,384]{4,2,1,0,3:T(8,128)S(1)} async-done(((f32[5,10,10,2,384]{4,2,1,0,3:T(8,128)}), f32[5,10,10,2,384]{4,2,1,0,3:T(8,128)S(1)}, u32[]{:S(2)}, u32[]{:S(2)}) %all-to-all-start.2) | async-done | bytes 1536032 | tf_op jit(solution)/shard_map/all_to_all | solution.py:154
  78.1 6.6 %all-to-all-start = ((f32[5,10,10,2,384]{4,2,1,0,3:T(8,128)}), f32[5,10,10,2,384]{4,2,1,0,3:T(8,128)}, u32[]{:S(2)}, u32[]{:S(2)}) async-start(f32[5,10,10,2,384]{4,2,1,0,3:T(8,128)} %get-tuple-element.44), calls=%async_computation | async-start | bytes 4915200 | tf_op jit(solution)/shard_map/all_to_all | solution.py:152
  84.7 2.2 copy.25
  86.9 3.7 fusion.130
  90.7 3.7 fusion.131
  94.3 15.7 %all-to-all-done = f32[5,10,10,2,384]{4,2,1,0,3:T(8,128)} async-done(((f32[5,10,10,2,384]{4,2,1,0,3:T(8,128)}), f32[5,10,10,2,384]{4,2,1,0,3:T(8,128)}, u32[]{:S(2)}, u32[]{:S(2)}) %all-to-all-start) | async-done | bytes 1536032 | tf_op jit(solution)/shard_map/all_to_all | solution.py:152
  110.0 7.6 %fusion.37 = f32[10,10,10,384]{3,0,2,1:T(8,128)S(1)} fusion(f32[10,10,384,10]{2,3,1,0:T(8,128)} %fusion.131, f32[10,10,384,10]{2,3,1,0:T(8,128)} %fusion.130, f32[10,10,1,1]{0,1,3,2:T(8,128)S(1)} %copy-done.11, f32[10,10,10,384]{3,2,1,0:T(8,128)} %bitcast.10), kind=kOutput, calls=%fused_computation.71 | convolution fusion | flops 46848000 | bytes 6144400 | tf_op jit(solution)/shard_map/ia,i...->a.../dot_general | solution.py:50
  117.7 2.9 fusion.38
  120.6 15.3 %reshape.219 = f32[10,10,10,6,8,8]{5,4,3,2,1,0:T(8,128)} reshape(f32[10,10,10,384]{3,2,1,0:T(8,128)S(1)} %fusion.38) | data formatting | bytes 3072000 | tf_op jit(solution)/shard_map/reshape | solution.py:165
  137.3 2.9 slice.174
  141.8 2.0 fusion.129
  143.8 1.9 fusion.128
  147.2 20.9 %select_add_fusion.2 = f32[10,10,10,6,8,8]{5,4,3,2,1,0:T(8,128)} fusion(f32[10,10,10,6,8,8]{5,4,3,2,1,0:T(8,128)} %reshape.219, f32[10,10,6,8,8]{4,3,2,1,0:T(8,128)S(1)} %get-tuple-element.63, f32[10,10,6,8,8]{4,3,2,1,0:T(8,128)S(1)} %get-tuple-element.61, pred[10]{0:T(512)(128)(4,1)S(1)} %iota_compare_fusion.5, pred[10]{0:T(512)(128)(4,1)S(1)} %iota_compare_fusion.6), kind=kLoop, calls=%fused_computation.2 | loop fusion | flops 1536000 | bytes 3379220 | tf_op jit(solution)/shard_map/add | solution.py:71
  168.2 5.9 %fusion.120 = (f32[10,1,10,6,7,8]{5,4,3,2,1,0:T(8,128)}, f32[10,1,10,6,7,8]{5,4,3,2,1,0:T(8,128)}) fusion(f32[10,10,10,6,8,8]{5,4,3,2,1,0:T(8,128)} %select_add_fusion.2), kind=kLoop, calls=%fused_computation.192 | loop fusion | bytes 537600 | tf_op jit(solution)/shard_map/slice | solution.py:67
  174.1 6.9 %fusion.123 = (f32[10,1,10,6,8,8]{5,4,3,2,1,0:T(8,128)}, f32[10,10,6,8,8]{4,3,2,1,0:T(8,128)}, f32[10,10,6,8,8]{4,3,2,1,0:T(8,128)}, f32[10,1,10,6,8,8]{5,4,3,2,1,0:T(8,128)}) fusion(f32[10,1,10,6,7,8]{5,4,3,2,1,0:T(8,128)} %get-tuple-element.33, f32[10,1,10,6,7,8]{5,4,3,2,1,0:T(8,128)} %get-tuple-element.34), kind=kLoop, calls=%fused_computation.195 | loop fusion | bytes 883200 | tf_op jit(solution)/shard_map/concatenate | solution.py:66
  181.0 14.5 %select_add_fusion.1 = f32[10,10,10,6,8,8]{5,4,3,2,1,0:T(8,128)} fusion(f32[10,10,6,8,8]{4,3,2,1,0:T(8,128)} %get-tuple-element.64, f32[10,10,6,8,8]{4,3,2,1,0:T(8,128)} %get-tuple-element.51, pred[10]{0:T(512)(128)(4,1)S(1)} %iota_compare_fusion.5, pred[10]{0:T(512)(128)(4,1)S(1)} %iota_compare_fusion.6, f32[10,10,6,8,8]{4,3,2,1,0:T(8,128)S(1)} %get-tuple-element.63, ...), kind=kLoop, calls=%fused_computation.1 | loop fusion | flops 3072000 | bytes 3686420 | tf_op jit(solution)/shard_map/add | solution.py:71
  195.5 3.3 fusion.119
  198.8 3.0 fusion.125
  201.8 2.7 fusion.126
  204.5 17.3 %select_add_fusion = f32[10,10,10,6,8,8]{5,4,3,2,1,0:T(8,128)} fusion(f32[10,10,6,8,8]{4,3,2,1,0:T(8,128)} %get-tuple-element.57, f32[10,10,6,8,8]{4,3,2,1,0:T(8,128)} %get-tuple-element.55, pred[10]{0:T(512)(128)(4,1)S(1)} %iota_compare_fusion.5, pred[10]{0:T(512)(128)(4,1)S(1)} %iota_compare_fusion.6, f32[10,10,6,8,8]{4,3,2,1,0:T(8,128)} %get-tuple-element.64, ...), kind=kLoop, calls=%fused_computation | loop fusion | flops 4608000 | bytes 3993620 | tf_op jit(solution)/shard_map/add | solution.py:71
  223.2 2.5 slice_reduce_fusion.11
  228.3 4.5 %slice_reduce_fusion.1 = (f32[10,10,6,8]{3,2,1,0:T(8,128)S(1)}, f32[10,10,6,8]{3,2,1,0:T(8,128)S(1)}) fusion(f32[10,10,10,6,8,8]{5,4,3,2,1,0:T(8,128)} %select_add_fusion), kind=kLoop, calls=%fused_computation.42 | loop fusion | bytes 76800 | tf_op jit(solution)/shard_map/slice | solution.py:96
  232.8 2.2 fusion.118
  235.0 5.0 %slice_reduce_fusion.3 = (f32[10,10,6,8]{3,2,1,0:T(8,128)}, f32[10,10,6,8]{3,2,1,0:T(8,128)}) fusion(f32[10,10,10,6,8,8]{5,4,3,2,1,0:T(8,128)} %select_add_fusion), kind=kLoop, calls=%fused_computation.143 | loop fusion | bytes 76800 | tf_op jit(solution)/shard_map/slice | solution.py:96
  241.3 3.6 broadcast_in_dim.442
  244.9 3.4 broadcast_in_dim.452
  250.2 3.9 broadcast_in_dim.460
  254.2 1.9 broadcast_in_dim.462
  256.1 9.8 %collective-permute-start = (f32[1]{0:T(128)}, f32[1]{0:T(128)}, u32[]{:S(2)}, u32[]{:S(2)}) collective-permute-start(f32[1]{0:T(128)} %bitcast.39), channel_id=1, source_target_pairs={{0,21},{1,22},{2,23},{3,24},{4,25},{5,26},{6,27},{7,28},{8,29},{9,... | collective-permute-start | bytes 20 | tf_op jit(solution)/shard_map/ppermute | solution.py:17
  269.8 6.9 %collective-permute-start.8 = (f32[1]{0:T(128)}, f32[1]{0:T(128)}, u32[]{:S(2)}, u32[]{:S(2)}) collective-permute-start(f32[1]{0:T(128)} %bitcast.48), channel_id=1, source_target_pairs={{0,11},{1,12},{2,13},{3,14},{4,15},{5,16},{6,17},{7,18},{8,19},{9,... | collective-permute-start | bytes 20 | tf_op jit(solution)/shard_map/ppermute | solution.py:17
  290.4 6.5 %collective-permute-start.6 = (f32[1]{0:T(128)}, f32[1]{0:T(128)}, u32[]{:S(2)}, u32[]{:S(2)}) collective-permute-start(f32[1]{0:T(128)} %bitcast.45), channel_id=1, source_target_pairs={{0,13},{1,14},{2,15},{3,16},{4,17},{5,18},{6,19},{7,20},{8,21},{9,... | collective-permute-start | bytes 20 | tf_op jit(solution)/shard_map/ppermute | solution.py:17
  297.6 2.9 collective-permute-start.2
  303.7 3.6 collective-permute-start.14
  310.5 4.5 %collective-permute-start.9 = (f32[60]{0:T(128)S(1)}, f32[60]{0:T(128)S(1)}, u32[]{:S(2)}, u32[]{:S(2)}) collective-permute-start(f32[60]{0:T(128)S(1)} %reshape.229), channel_id=1, source_target_pairs={{0,5},{1,6},{2,7},{3,8},{4,9},{5,10},{6,11},{7,12},{8,13},{9,14},{... | collective-permute-start | bytes 728 | tf_op jit(solution)/shard_map/ppermute | solution.py:17
  320.8 7.9 %collective-permute-start.3 = (f32[80]{0:T(128)S(1)}, f32[80]{0:T(128)S(1)}, u32[]{:S(2)}, u32[]{:S(2)}) collective-permute-start(f32[80]{0:T(128)S(1)} %reshape.223), channel_id=1, source_target_pairs={{0,17},{1,18},{2,19},{3,20},{4,21},{5,22},{6,23},{7,24},{8,25},{9,... | collective-permute-start | bytes 968 | tf_op jit(solution)/shard_map/ppermute | solution.py:17
  336.5 6.7 %collective-permute-start.1 = (f32[80]{0:T(128)S(1)}, f32[80]{0:T(128)S(1)}, u32[]{:S(2)}, u32[]{:S(2)}) collective-permute-start(f32[80]{0:T(128)S(1)} %reshape.221), channel_id=1, source_target_pairs={{0,20},{1,21},{2,22},{3,23},{4,24},{5,25},{6,26},{7,27},{8,28},{9,... | collective-permute-start | bytes 968 | tf_op jit(solution)/shard_map/ppermute | solution.py:17
  345.2 5.4 %collective-permute-start.12 = (f32[4800]{0:T(1024)S(1)}, f32[4800]{0:T(1024)S(1)}, u32[]{:S(2)}, u32[]{:S(2)}) collective-permute-start(f32[4800]{0:T(1024)S(1)} %reshape.232), channel_id=1, source_target_pairs={{0,1},{1,2},{2,3},{3,4},{4,5},{5,6},{6,7},{7,8},{8,9},{9,10},{10,1... | collective-permute-start | bytes 57608 | tf_op jit(solution)/shard_map/ppermute | solution.py:17
  352.6 4.3 %collective-permute-start.10 = (f32[4800]{0:T(1024)S(1)}, f32[4800]{0:T(1024)S(1)}, u32[]{:S(2)}, u32[]{:S(2)}) collective-permute-start(f32[4800]{0:T(1024)S(1)} %reshape.230), channel_id=1, source_target_pairs={{0,4},{1,5},{2,6},{3,7},{4,8},{5,9},{6,10},{7,11},{8,12},{9,13},{1... | collective-permute-start | bytes 57608 | tf_op jit(solution)/shard_map/ppermute | solution.py:17
  365.3 5.6 %collective-permute-start.4 = (f32[6400]{0:T(1024)}, f32[6400]{0:T(1024)}, u32[]{:S(2)}, u32[]{:S(2)}) collective-permute-start(f32[6400]{0:T(1024)} %reshape.224), channel_id=1, source_target_pairs={{0,16},{1,17},{2,18},{3,19},{4,20},{5,21},{6,22},{7,23},{8,24},{9,... | collective-permute-start | bytes 76808 | tf_op jit(solution)/shard_map/ppermute | solution.py:17
  380.2 1.9 broadcast_in_dim.518
  389.2 3.8 broadcast_in_dim.484
  393.2 13.5 %fusion.61 = f32[10,10,10,1,384]{4,2,1,0,3:T(8,128)S(1)} fusion(f32[10,10,10,384]{3,2,1,0:T(8,128)S(1)} %copy-done.3, f32[]{:T(128)} %bitcast.61, f32[10,384]{1,0:T(8,128)S(1)} %copy-done.17, f32[]{:T(128)} %bitcast.58, f32[10,384]{1,0:T(8,128)S(1)} %copy-done.21, f32[10,10,384]{2,1,0:T(8,128)} %broadcast_in_dim.546, f32[10,384]{1,0:T(8,128)S(1)} %copy-done.22, ...), kind=kOutput, calls=%fused_computation.94 | convolution fusion | flops 1811859456 | bytes 5103412 | tf_op jit(solution)/shard_map/abcj,ij->abci/dot_general | solution.py:185
  406.7 2.7 copy.32
  (246 shorter events, 77.0 us)
Async XLA Ops:
  46.9 31.2 %all-to-all-start.2 = ((f32[5,10,10,2,384]{4,2,1,0,3:T(8,128)}), f32[5,10,10,2,384]{4,2,1,0,3:T(8,128)S(1)}, u32[]{:S(2)}, u32[]{:S(2)}) async-start(f32[5,10,10,2,384]{4,2,1,0,3:T(8,128)} %get-tuple-element.46), calls=%async_computation.2 | async-start | bytes 4915200 | tf_op jit(solution)/shard_map/all_to_all | solution.py:154
  52.0 65.6 %copy-start.28 = (s32[384]{0:T(512)}, s32[384]{0:T(512)S(1)}, u32[]{:S(2)}) copy-start(s32[384]{0:T(512)S(1)} %reduce) | copy-start | bytes 4612
  56.3 148.2 %copy-start.24 = (pred[10]{0:T(512)(128)(4,1)}, pred[10]{0:T(512)(128)(4,1)S(1)}, u32[]{:S(2)}) copy-start(pred[10]{0:T(512)(128)(4,1)S(1)} %iota_compare_fusion.6) | copy-start | bytes 34
  78.1 31.9 %all-to-all-start = ((f32[5,10,10,2,384]{4,2,1,0,3:T(8,128)}), f32[5,10,10,2,384]{4,2,1,0,3:T(8,128)}, u32[]{:S(2)}, u32[]{:S(2)}) async-start(f32[5,10,10,2,384]{4,2,1,0,3:T(8,128)} %get-tuple-element.44), calls=%async_computation | async-start | bytes 4915200 | tf_op jit(solution)/shard_map/all_to_all | solution.py:152
  84.7 119.8 %copy-start.26 = (pred[10]{0:T(512)(128)(4,1)}, pred[10]{0:T(512)(128)(4,1)S(1)}, u32[]{:S(2)}) copy-start(pred[10]{0:T(512)(128)(4,1)S(1)} %iota_compare_fusion.5) | copy-start | bytes 34
  120.6 15.4 %copy-start.2 = (f32[10,10,10,384]{3,2,1,0:T(8,128)}, f32[10,10,10,384]{3,2,1,0:T(8,128)S(1)}, u32[]{:S(2)}) copy-start(f32[10,10,10,384]{3,2,1,0:T(8,128)S(1)} %fusion.38) | copy-start | bytes 4608004
  147.2 33.7 %slice-start = ((s8[24576000]{0:T(1024)(128)(4,1)}), s8[4194304]{0:T(1024)(128)(4,1)S(1)}, s32[]{:S(2)}) async-start(s8[24576000]{0:T(1024)(128)(4,1)} %bitcast.222), calls=%async_computation.3 | async-start | bytes 8388608
  147.2 33.8 %slice-start.1 = ((s8[24576000]{0:T(1024)(128)(4,1)}), s8[4194304]{0:T(1024)(128)(4,1)S(1)}, s32[]{:S(2)}) async-start(s8[24576000]{0:T(1024)(128)(4,1)} %bitcast.222), calls=%async_computation.4 | async-start | bytes 8388608
  147.2 33.8 %slice-start.2 = ((s8[24576000]{0:T(1024)(128)(4,1)}), s8[4194304]{0:T(1024)(128)(4,1)S(1)}, s32[]{:S(2)}) async-start(s8[24576000]{0:T(1024)(128)(4,1)} %bitcast.222), calls=%async_computation.5 | async-start | bytes 8388608
  147.2 33.8 %slice-start.3 = ((s8[24576000]{0:T(1024)(128)(4,1)}), s8[4194304]{0:T(1024)(128)(4,1)S(1)}, s32[]{:S(2)}) async-start(s8[24576000]{0:T(1024)(128)(4,1)} %bitcast.222), calls=%async_computation.6 | async-start | bytes 8388608
  147.2 33.8 %slice-start.4 = ((s8[24576000]{0:T(1024)(128)(4,1)}), s8[4194304]{0:T(1024)(128)(4,1)S(1)}, s32[]{:S(2)}) async-start(s8[24576000]{0:T(1024)(128)(4,1)} %bitcast.222), calls=%async_computation.7 | async-start | bytes 8388608
  174.1 6.9 %slice-start.5 = ((s8[24576000]{0:T(1024)(128)(4,1)}), s8[3604480]{0:T(1024)(128)(4,1)S(1)}, s32[]{:S(2)}) async-start(s8[24576000]{0:T(1024)(128)(4,1)} %bitcast.222), calls=%async_computation.8 | async-start | bytes 7208960
  232.8 7.3 %copy-start.6 = (f32[1,10,10,6,8,8]{5,4,3,0,2,1:T(8,128)S(1)}, f32[1,10,10,6,8,8]{5,4,3,0,2,1:T(8,128)}, u32[]{:S(2)}) copy-start(f32[1,10,10,6,8,8]{5,4,3,0,2,1:T(8,128)} %get-tuple-element.62) | copy-start | bytes 460804
  241.3 7.0 %copy-start.4 = (f32[10,1,10,6,8,8]{5,4,3,2,1,0:T(8,128)S(1)}, f32[10,1,10,6,8,8]{5,4,3,2,1,0:T(8,128)}, u32[]{:S(2)}) copy-start(f32[10,1,10,6,8,8]{5,4,3,2,1,0:T(8,128)} %get-tuple-element.65) | copy-start | bytes 460804
  256.1 31.6 %copy-start.8 = (f32[1,10,10,1,8,8]{5,4,3,2,1,0:T(8,128)S(1)}, f32[1,10,10,1,8,8]{5,4,3,2,1,0:T(8,128)}, u32[]{:S(2)}) copy-start(f32[1,10,10,1,8,8]{5,4,3,2,1,0:T(8,128)} %get-tuple-element.30) | copy-start | bytes 76804
  256.1 32.5 %collective-permute-start = (f32[1]{0:T(128)}, f32[1]{0:T(128)}, u32[]{:S(2)}, u32[]{:S(2)}) collective-permute-start(f32[1]{0:T(128)} %bitcast.39), channel_id=1, source_target_pairs={{0,21},{1,22},{2,23},{3,24},{4,25},{5,26},{6,27},{7,28},{8,29},{9,... | collective-permute-start | bytes 20 | tf_op jit(solution)/shard_map/ppermute | solution.py:17
  265.9 24.5 %collective-permute-start.25 = (f32[1]{0:T(128)}, f32[1]{0:T(128)}, u32[]{:S(2)}, u32[]{:S(2)}) collective-permute-start(f32[1]{0:T(128)} %bitcast.60), channel_id=1, source_target_pairs={{21,0},{22,1},{23,2},{24,3},{25,4},{26,5},{27,6},{28,7},{29,8},{30... | collective-permute-start | bytes 20 | tf_op jit(solution)/shard_map/ppermute | solution.py:17
  267.2 30.4 %collective-permute-start.19 = (f32[1]{0:T(128)}, f32[1]{0:T(128)}, u32[]{:S(2)}, u32[]{:S(2)}) collective-permute-start(f32[1]{0:T(128)} %bitcast.54), channel_id=1, source_target_pairs={{13,0},{14,1},{15,2},{16,3},{17,4},{18,5},{19,6},{20,7},{21,8},{22... | collective-permute-start | bytes 20 | tf_op jit(solution)/shard_map/ppermute | solution.py:17
  268.5 32.6 %collective-permute-start.17 = (f32[1]{0:T(128)}, f32[1]{0:T(128)}, u32[]{:S(2)}, u32[]{:S(2)}) collective-permute-start(f32[1]{0:T(128)} %bitcast.51), channel_id=1, source_target_pairs={{11,0},{12,1},{13,2},{14,3},{15,4},{16,5},{17,6},{18,7},{19,8},{20... | collective-permute-start | bytes 20 | tf_op jit(solution)/shard_map/ppermute | solution.py:17
  269.8 33.9 %collective-permute-start.8 = (f32[1]{0:T(128)}, f32[1]{0:T(128)}, u32[]{:S(2)}, u32[]{:S(2)}) collective-permute-start(f32[1]{0:T(128)} %bitcast.48), channel_id=1, source_target_pairs={{0,11},{1,12},{2,13},{3,14},{4,15},{5,16},{6,17},{7,18},{8,19},{9,... | collective-permute-start | bytes 20 | tf_op jit(solution)/shard_map/ppermute | solution.py:17
  288.6 19.4 %collective-permute-start.23 = (f32[1]{0:T(128)}, f32[1]{0:T(128)}, u32[]{:S(2)}, u32[]{:S(2)}) collective-permute-start(f32[1]{0:T(128)} %bitcast.57), channel_id=1, source_target_pairs={{19,0},{20,1},{21,2},{22,3},{23,4},{24,5},{25,6},{26,7},{27,8},{28... | collective-permute-start | bytes 20 | tf_op jit(solution)/shard_map/ppermute | solution.py:17
  290.4 20.1 %collective-permute-start.6 = (f32[1]{0:T(128)}, f32[1]{0:T(128)}, u32[]{:S(2)}, u32[]{:S(2)}) collective-permute-start(f32[1]{0:T(128)} %bitcast.45), channel_id=1, source_target_pairs={{0,13},{1,14},{2,15},{3,16},{4,17},{5,18},{6,19},{7,20},{8,21},{9,... | collective-permute-start | bytes 20 | tf_op jit(solution)/shard_map/ppermute | solution.py:17
  297.6 18.1 %collective-permute-start.2 = (f32[1]{0:T(128)}, f32[1]{0:T(128)}, u32[]{:S(2)}, u32[]{:S(2)}) collective-permute-start(f32[1]{0:T(128)} %bitcast.42), channel_id=1, source_target_pairs={{0,19},{1,20},{2,21},{3,22},{4,23},{5,24},{6,25},{7,26},{8,27},{9,... | collective-permute-start | bytes 20 | tf_op jit(solution)/shard_map/ppermute | solution.py:17
  301.1 17.0 %collective-permute-start.11 = (f32[60]{0:T(128)S(1)}, f32[60]{0:T(128)S(1)}, u32[]{:S(2)}, u32[]{:S(2)}) collective-permute-start(f32[60]{0:T(128)S(1)} %reshape.231), channel_id=1, source_target_pairs={{0,3},{1,4},{2,5},{3,6},{4,7},{5,8},{6,9},{7,10},{8,11},{9,12},{10... | collective-permute-start | bytes 728 | tf_op jit(solution)/shard_map/ppermute | solution.py:17
  303.7 15.7 %collective-permute-start.14 = (f32[60]{0:T(128)S(1)}, f32[60]{0:T(128)S(1)}, u32[]{:S(2)}, u32[]{:S(2)}) collective-permute-start(f32[60]{0:T(128)S(1)} %reshape.234), channel_id=1, source_target_pairs={{3,0},{4,1},{5,2},{6,3},{7,4},{8,5},{9,6},{10,7},{11,8},{12,9},{13... | collective-permute-start | bytes 728 | tf_op jit(solution)/shard_map/ppermute | solution.py:17
  308.0 12.8 %collective-permute-start.16 = (f32[60]{0:T(128)S(1)}, f32[60]{0:T(128)S(1)}, u32[]{:S(2)}, u32[]{:S(2)}) collective-permute-start(f32[60]{0:T(128)S(1)} %reshape.236), channel_id=1, source_target_pairs={{5,0},{6,1},{7,2},{8,3},{9,4},{10,5},{11,6},{12,7},{13,8},{14,9},{... | collective-permute-start | bytes 728 | tf_op jit(solution)/shard_map/ppermute | solution.py:17
  310.5 18.4 %collective-permute-start.9 = (f32[60]{0:T(128)S(1)}, f32[60]{0:T(128)S(1)}, u32[]{:S(2)}, u32[]{:S(2)}) collective-permute-start(f32[60]{0:T(128)S(1)} %reshape.229), channel_id=1, source_target_pairs={{0,5},{1,6},{2,7},{3,8},{4,9},{5,10},{6,11},{7,12},{8,13},{9,14},{... | collective-permute-start | bytes 728 | tf_op jit(solution)/shard_map/ppermute | solution.py:17
  315.7 18.1 %collective-permute-start.5 = (f32[80]{0:T(128)S(1)}, f32[80]{0:T(128)S(1)}, u32[]{:S(2)}, u32[]{:S(2)}) collective-permute-start(f32[80]{0:T(128)S(1)} %reshape.225), channel_id=1, source_target_pairs={{0,15},{1,16},{2,17},{3,18},{4,19},{5,20},{6,21},{7,22},{8,23},{9,... | collective-permute-start | bytes 968 | tf_op jit(solution)/shard_map/ppermute | solution.py:17
  318.2 17.0 %collective-permute-start.20 = (f32[80]{0:T(128)S(1)}, f32[80]{0:T(128)S(1)}, u32[]{:S(2)}, u32[]{:S(2)}) collective-permute-start(f32[80]{0:T(128)S(1)} %reshape.240), channel_id=1, source_target_pairs={{15,0},{16,1},{17,2},{18,3},{19,4},{20,5},{21,6},{22,7},{23,8},{24... | collective-permute-start | bytes 968 | tf_op jit(solution)/shard_map/ppermute | solution.py:17
  319.5 17.0 %collective-permute-start.22 = (f32[80]{0:T(128)S(1)}, f32[80]{0:T(128)S(1)}, u32[]{:S(2)}, u32[]{:S(2)}) collective-permute-start(f32[80]{0:T(128)S(1)} %reshape.242), channel_id=1, source_target_pairs={{17,0},{18,1},{19,2},{20,3},{21,4},{22,5},{23,6},{24,7},{25,8},{26... | collective-permute-start | bytes 968 | tf_op jit(solution)/shard_map/ppermute | solution.py:17
  320.8 22.4 %collective-permute-start.3 = (f32[80]{0:T(128)S(1)}, f32[80]{0:T(128)S(1)}, u32[]{:S(2)}, u32[]{:S(2)}) collective-permute-start(f32[80]{0:T(128)S(1)} %reshape.223), channel_id=1, source_target_pairs={{0,17},{1,18},{2,19},{3,20},{4,21},{5,22},{6,23},{7,24},{8,25},{9,... | collective-permute-start | bytes 968 | tf_op jit(solution)/shard_map/ppermute | solution.py:17
  328.9 16.2 %collective-permute-start.7 = (f32[80]{0:T(128)S(1)}, f32[80]{0:T(128)S(1)}, u32[]{:S(2)}, u32[]{:S(2)}) collective-permute-start(f32[80]{0:T(128)S(1)} %reshape.227), channel_id=1, source_target_pairs={{0,12},{1,13},{2,14},{3,15},{4,16},{5,17},{6,18},{7,19},{8,20},{9,... | collective-permute-start | bytes 968 | tf_op jit(solution)/shard_map/ppermute | solution.py:17
  333.8 16.8 %collective-permute-start.18 = (f32[80]{0:T(128)S(1)}, f32[80]{0:T(128)S(1)}, u32[]{:S(2)}, u32[]{:S(2)}) collective-permute-start(f32[80]{0:T(128)S(1)} %reshape.238), channel_id=1, source_target_pairs={{12,0},{13,1},{14,2},{15,3},{16,4},{17,5},{18,6},{19,7},{20,8},{21... | collective-permute-start | bytes 968 | tf_op jit(solution)/shard_map/ppermute | solution.py:17
  335.2 17.4 %collective-permute-start.24 = (f32[80]{0:T(128)S(1)}, f32[80]{0:T(128)S(1)}, u32[]{:S(2)}, u32[]{:S(2)}) collective-permute-start(f32[80]{0:T(128)S(1)} %reshape.244), channel_id=1, source_target_pairs={{20,0},{21,1},{22,2},{23,3},{24,4},{25,5},{26,6},{27,7},{28,8},{29... | collective-permute-start | bytes 968 | tf_op jit(solution)/shard_map/ppermute | solution.py:17
  336.5 20.4 %collective-permute-start.1 = (f32[80]{0:T(128)S(1)}, f32[80]{0:T(128)S(1)}, u32[]{:S(2)}, u32[]{:S(2)}) collective-permute-start(f32[80]{0:T(128)S(1)} %reshape.221), channel_id=1, source_target_pairs={{0,20},{1,21},{2,22},{3,23},{4,24},{5,25},{6,26},{7,27},{8,28},{9,... | collective-permute-start | bytes 968 | tf_op jit(solution)/shard_map/ppermute | solution.py:17
  343.2 22.1 %collective-permute-start.13 = (f32[4800]{0:T(1024)S(1)}, f32[4800]{0:T(1024)S(1)}, u32[]{:S(2)}, u32[]{:S(2)}) collective-permute-start(f32[4800]{0:T(1024)S(1)} %reshape.233), channel_id=1, source_target_pairs={{1,0},{2,1},{3,2},{4,3},{5,4},{6,5},{7,6},{8,7},{9,8},{10,9},{11,1... | collective-permute-start | bytes 57608 | tf_op jit(solution)/shard_map/ppermute | solution.py:17
  345.2 25.8 %collective-permute-start.12 = (f32[4800]{0:T(1024)S(1)}, f32[4800]{0:T(1024)S(1)}, u32[]{:S(2)}, u32[]{:S(2)}) collective-permute-start(f32[4800]{0:T(1024)S(1)} %reshape.232), channel_id=1, source_target_pairs={{0,1},{1,2},{2,3},{3,4},{4,5},{5,6},{6,7},{7,8},{8,9},{9,10},{10,1... | collective-permute-start | bytes 57608 | tf_op jit(solution)/shard_map/ppermute | solution.py:17
  350.6 20.4 %collective-permute-start.15 = (f32[4800]{0:T(1024)S(1)}, f32[4800]{0:T(1024)S(1)}, u32[]{:S(2)}, u32[]{:S(2)}) collective-permute-start(f32[4800]{0:T(1024)S(1)} %reshape.235), channel_id=1, source_target_pairs={{4,0},{5,1},{6,2},{7,3},{8,4},{9,5},{10,6},{11,7},{12,8},{13,9},{1... | collective-permute-start | bytes 57608 | tf_op jit(solution)/shard_map/ppermute | solution.py:17
  352.6 18.4 %collective-permute-start.10 = (f32[4800]{0:T(1024)S(1)}, f32[4800]{0:T(1024)S(1)}, u32[]{:S(2)}, u32[]{:S(2)}) collective-permute-start(f32[4800]{0:T(1024)S(1)} %reshape.230), channel_id=1, source_target_pairs={{0,4},{1,5},{2,6},{3,7},{4,8},{5,9},{6,10},{7,11},{8,12},{9,13},{1... | collective-permute-start | bytes 57608 | tf_op jit(solution)/shard_map/ppermute | solution.py:17
  356.9 28.2 %collective-permute-start.21 = (f32[6400]{0:T(1024)}, f32[6400]{0:T(1024)S(1)}, u32[]{:S(2)}, u32[]{:S(2)}) collective-permute-start(f32[6400]{0:T(1024)} %reshape.241), channel_id=1, source_target_pairs={{16,0},{17,1},{18,2},{19,3},{20,4},{21,5},{22,6},{23,7},{24,8},{25... | collective-permute-start | bytes 76808 | tf_op jit(solution)/shard_map/ppermute | solution.py:17
  365.3 19.5 %collective-permute-start.4 = (f32[6400]{0:T(1024)}, f32[6400]{0:T(1024)}, u32[]{:S(2)}, u32[]{:S(2)}) collective-permute-start(f32[6400]{0:T(1024)} %reshape.224), channel_id=1, source_target_pairs={{0,16},{1,17},{2,18},{3,19},{4,20},{5,21},{6,22},{7,23},{8,24},{9,... | collective-permute-start | bytes 76808 | tf_op jit(solution)/shard_map/ppermute | solution.py:17
  387.4 5.6 %copy-start.14 = (f32[10,384]{1,0:T(8,128)S(1)}, f32[10,384]{1,0:T(8,128)}, u32[]{:S(2)}) copy-start(f32[10,384]{1,0:T(8,128)} %broadcast_in_dim.522) | copy-start | bytes 46084
  387.5 5.6 %copy-start.15 = (f32[10,384]{1,0:T(8,128)S(1)}, f32[10,384]{1,0:T(8,128)}, u32[]{:S(2)}) copy-start(f32[10,384]{1,0:T(8,128)} %broadcast_in_dim.510) | copy-start | bytes 46084
  387.5 5.6 %copy-start.16 = (f32[10,384]{1,0:T(8,128)S(1)}, f32[10,384]{1,0:T(8,128)}, u32[]{:S(2)}) copy-start(f32[10,384]{1,0:T(8,128)} %broadcast_in_dim.473) | copy-start | bytes 46084
  387.5 5.6 %copy-start.17 = (f32[10,384]{1,0:T(8,128)S(1)}, f32[10,384]{1,0:T(8,128)}, u32[]{:S(2)}) copy-start(f32[10,384]{1,0:T(8,128)} %broadcast_in_dim.556) | copy-start | bytes 46084
  387.5 5.6 %copy-start.18 = (f32[10,384]{1,0:T(8,128)S(1)}, f32[10,384]{1,0:T(8,128)}, u32[]{:S(2)}) copy-start(f32[10,384]{1,0:T(8,128)} %broadcast_in_dim.536) | copy-start | bytes 46084
  387.5 5.6 %copy-start.25 = (pred[10]{0:T(512)(128)(4,1)S(1)}, pred[10]{0:T(512)(128)(4,1)}, u32[]{:S(2)}) copy-start(pred[10]{0:T(512)(128)(4,1)} %copy-done.24) | copy-start | bytes 34
  387.5 5.6 %copy-start.27 = (pred[10]{0:T(512)(128)(4,1)S(1)}, pred[10]{0:T(512)(128)(4,1)}, u32[]{:S(2)}) copy-start(pred[10]{0:T(512)(128)(4,1)} %copy-done.26) | copy-start | bytes 34
  (25 other events, 102.4 us)
where the time goes:
time: 417 us; the launch traced here: 410 us
  local copies, waits for them, and re-layouts  148 us (35%)
  starting transfers between devices  98.2 us (24%)
  other arithmetic  57.4 us (14%)
  waiting for transfers between devices  37.5 us (9%)
  matrix products  31.4 us (8%)
  blocking collectives  30.7 us (7%)
  between operations  6.53 us (2%)
    ppermute x26, starting transfers between devices, passed_along(): return lax.ppermute(x, axis, pairs)  86.5 us
    add x3, other arithmetic, local_pass(): return field + jnp.where(node_iota == last_node, add_upper, 0.0)  52.7 us
    broadcast_in_dim x54, local copies, waits for them, and re-layouts, add_region(): jnp.where(region_mask(field.shape, offset, block_grid), values, 0.0)  32.5 us
    all_to_all x1, blocking collectives, body(): lax.all_to_all(fluxes[1], 'comp', split_axis=3, concat_axis=0, tiled=True)  30.7 us
    all_to_all x1, waiting for transfers between devices, body(): lax.all_to_all(fluxes[2], 'comp', split_axis=3, concat_axis=0, tiled=True)  21.8 us
    slice x7, local copies, waits for them, and re-layouts, take_region(): return field[nodes_key + elems_key]  18.2 us
    all_to_all x1, waiting for transfers between devices, body(): lax.all_to_all(fluxes[0], 'comp', split_axis=3, concat_axis=0, tiled=True)  15.7 us
    reshape x1, local copies, waits for them, and re-layouts, body(): canonical.reshape((node_count, node_count, node_count) + block_grid)  15.3 us
  transfers between devices with their start and end apart: 28, of which 2 were waited for; matrix products, arithmetic and copies ran while one was open for 12% of the time, Pallas kernels for 0%

commit v1 on v0

--- a/solution.py
+++ b/solution.py
@@ -149,7 +149,12 @@
             + geometry[2, direction] * velocity[2]
         )
     flux_r, flux_s, flux_t = (
-        lax.all_to_all(fluxes[0], "comp", split_axis=3, concat_axis=0, tiled=True),
+        jnp.concatenate(
+            lax.all_to_all(
+                jnp.stack(jnp.split(fluxes[0], lax.axis_size("comp"), axis=3)), "comp", 0, 0
+            ),
+            axis=0,
+        ),
         lax.all_to_all(fluxes[1], "comp", split_axis=3, concat_axis=0, tiled=True),
         lax.all_to_all(fluxes[2], "comp", split_axis=3, concat_axis=0, tiled=True),
     )

time: 417 us -> 403 us (0.966)
  blocking collectives: 30.7 us -> 0 us
  waiting for transfers between devices: 37.5 us -> 45.9 us
  other arithmetic: 57.4 us -> 65.5 us
  starting transfers between devices: 98.2 us -> 103 us
    all_to_all x1 -> x0, blocking collectives: 30.7 us -> none  [body(): lax.all_to_all(fluxes[1], 'comp', split_axis=3, concat_axis=0, tiled=True)]
    slice x2 -> x0, local copies, waits for them, and re-layouts: 11.7 us -> none  [the longest x1 7.84 us: body(): geometry[0, direction] * velocity[0] + geometry[1, direction] * velocity[1]]
    all_to_all x1 -> x2, waiting for transfers between devices: 15.7 us -> 22.1 us  [the longest x1 16.2 us: body(): lax.all_to_all(fluxes[1], 'comp', split_axis=3, concat_axis=0, tiled=True)]
    all_to_all x1 -> x2, starting transfers between devices: 6.57 us -> 12.4 us  [the longest x1 6.2 us: body(): lax.all_to_all(jnp.stack(jnp.split(fluxes[0], lax.axis_size('comp'), axis...]
    add x1, other arithmetic: 4.47 us -> 9.91 us  [body(): geometry[0, direction] * velocity[0] + geometry[1, direction] * velocity[1]]
    add x0 -> x2, local copies, waits for them, and re-layouts: none -> 4.86 us  [body(): geometry[0, direction] * velocity[0] + geometry[1, direction] * velocity[1]]
  transfers between devices with their start and end apart: 28 -> 29, of which waited for: 2 -> 3; matrix products, arithmetic and copies ran while one was open for 12% -> 15% of each run, Pallas kernels for 0% -> 0%
where the time goes in v1:
time: 403 us; the launch traced here: 396 us
  local copies, waits for them, and re-layouts  146 us (36%)
  starting transfers between devices  103 us (26%)
  other arithmetic  65.5 us (16%)
  waiting for transfers between devices  45.9 us (11%)
  matrix products  29.9 us (7%)
  between operations  6.44 us (2%)
    ppermute x26, starting transfers between devices, passed_along(): return lax.ppermute(x, axis, pairs)  86.4 us
    add x3, other arithmetic, local_pass(): return field + jnp.where(node_iota == last_node, add_upper, 0.0)  52.8 us
    broadcast_in_dim x54, local copies, waits for them, and re-layouts, add_region(): jnp.where(region_mask(field.shape, offset, block_grid), values, 0.0)  32.5 us
    all_to_all x1, waiting for transfers between devices, body(): lax.all_to_all(fluxes[2], 'comp', split_axis=3, concat_axis=0, tiled=True)  23.8 us
    slice x7, local copies, waits for them, and re-layouts, take_region(): return field[nodes_key + elems_key]  18.2 us
    all_to_all x1, waiting for transfers between devices, body(): lax.all_to_all(fluxes[1], 'comp', split_axis=3, concat_axis=0, tiled=True)  16.2 us
    reshape x1, local copies, waits for them, and re-layouts, body(): canonical.reshape((node_count, node_count, node_count) + block_grid)  15.4 us
    dot_general x1, matrix products, body(): jnp.einsum('abcj,ij->abci', assembled, place_matrix, precision=exact_mode)  13.5 us
  transfers between devices with their start and end apart: 29, of which 3 were waited for; matrix products, arithmetic and copies ran while one was open for 15% of the time, Pallas kernels for 0%

profile of v1, /device:TPU:7, one launch (start us, length us, event | category | flops | bytes accessed | tf_op | source)
XLA Modules:
  0.0 396.4 jit_solution(5952678448692855398)
XLA Ops:
  0.0 9.9 %fusion.55 = (f32[5,10,10,2,384]{4,3,2,1,0:T(2,128)}, f32[5,10,10,2,384]{4,3,2,1,0:T(2,128)S(1)}, f32[5,10,10,2,384]{4,3,2,1,0:T(2,128)}) fusion(f32[3,3,5,10,10,2,384]{6,5,4,3,2,1,0:T(2,128)} %param.5, f32[3,5,10,10,2,384]{5,4,3,2,1,0:T(2,128)} %param.4), kind=kLoop, calls=%fused_computation.80 | loop fusion | flops 5760000 | bytes 23040000 | tf_op jit(solution)/shard_map/add | solution.py:147
  11.6 4.1 %all-to-all-start.2 = ((f32[5,10,10,2,384]{4,2,1,0,3:T(8,128)}), f32[5,10,10,2,384]{4,2,1,0,3:T(8,128)S(1)}, u32[]{:S(2)}, u32[]{:S(2)}) async-start(f32[5,10,10,2,384]{4,2,1,0,3:T(8,128)} %copy.45), calls=%async_computation.2 | async-start | bytes 4915200 | tf_op jit(solution)/shard_map/all_to_all | solution.py:159
  15.7 3.2 copy.42
  18.9 23.8 %all-to-all-done.2 = f32[5,10,10,2,384]{4,2,1,0,3:T(8,128)S(1)} async-done(((f32[5,10,10,2,384]{4,2,1,0,3:T(8,128)}), f32[5,10,10,2,384]{4,2,1,0,3:T(8,128)S(1)}, u32[]{:S(2)}, u32[]{:S(2)}) %all-to-all-start.2) | async-done | bytes 1536032 | tf_op jit(solution)/shard_map/all_to_all | solution.py:159
  42.6 6.2 %all-to-all-start.1 = ((f32[5,10,10,2,384]{4,2,1,0,3:T(8,128)}), f32[5,10,10,2,384]{4,2,1,0,3:T(8,128)}, u32[]{:S(2)}, u32[]{:S(2)}) async-start(f32[5,10,10,2,384]{4,2,1,0,3:T(8,128)} %copy.42), calls=%async_computation.1 | async-start | bytes 4915200 | tf_op jit(solution)/shard_map/all_to_all | solution.py:158
  53.0 3.2 slice_bitcast_fusion.1
  56.2 2.6 pad_maximum_fusion
  58.8 16.2 %all-to-all-done.1 = f32[5,10,10,2,384]{4,2,1,0,3:T(8,128)} async-done(((f32[5,10,10,2,384]{4,2,1,0,3:T(8,128)}), f32[5,10,10,2,384]{4,2,1,0,3:T(8,128)}, u32[]{:S(2)}, u32[]{:S(2)}) %all-to-all-start.1) | async-done | bytes 1536032 | tf_op jit(solution)/shard_map/all_to_all | solution.py:158
  75.0 6.2 %all-to-all-start = ((f32[2,5,10,10,1,384]{5,4,3,2,1,0:T(1,128)}), f32[2,5,10,10,1,384]{5,4,3,2,1,0:T(1,128)}, u32[]{:S(2)}, u32[]{:S(2)}) async-start(f32[2,5,10,10,1,384]{5,4,3,2,1,0:T(1,128)} %pad_maximum_fusion), calls=%async_computation | async-start | bytes 3072000 | tf_op jit(solution)/shard_map/all_to_all | solution.py:153
  81.2 2.2 copy.43
  83.5 3.6 fusion.120
  87.1 3.7 fusion.119
  90.8 5.9 %all-to-all-done = f32[2,5,10,10,1,384]{5,4,3,2,1,0:T(1,128)} async-done(((f32[2,5,10,10,1,384]{5,4,3,2,1,0:T(1,128)}), f32[2,5,10,10,1,384]{5,4,3,2,1,0:T(1,128)}, u32[]{:S(2)}, u32[]{:S(2)}) %all-to-all-start) | async-done | bytes 1536032 | tf_op jit(solution)/shard_map/all_to_all | solution.py:153
  98.3 6.2 %fusion.22 = f32[10,10,10,384]{3,0,2,1:T(8,128)S(1)} fusion(f32[10,10,384,10]{2,3,1,0:T(8,128)S(1)} %copy-done.7, f32[10,10,384,10]{2,3,1,0:T(8,128)} %fusion.119, f32[10,10,1,1]{0,1,3,2:T(8,128)S(1)} %copy-done.12, f32[10,10,10,384]{3,2,1,0:T(8,128)S(1)} %bitcast.195), kind=kOutput, calls=%fused_computation.44 | convolution fusion | flops 46848000 | bytes 6144400 | tf_op jit(solution)/shard_map/ia,i...->a.../dot_general | solution.py:50
  104.5 2.9 fusion.23
  107.5 15.4 %reshape.220 = f32[10,10,10,6,8,8]{5,4,3,2,1,0:T(8,128)} reshape(f32[10,10,10,384]{3,2,1,0:T(8,128)S(1)} %fusion.23) | data formatting | bytes 3072000 | tf_op jit(solution)/shard_map/reshape | solution.py:170
  124.2 2.9 slice.174
  128.6 2.0 fusion.118
  130.7 2.0 fusion.117
  134.1 20.9 %select_add_fusion.2 = f32[10,10,10,6,8,8]{5,4,3,2,1,0:T(8,128)} fusion(f32[10,10,10,6,8,8]{5,4,3,2,1,0:T(8,128)} %reshape.220, f32[10,10,6,8,8]{4,3,2,1,0:T(8,128)S(1)} %get-tuple-element.51, f32[10,10,6,8,8]{4,3,2,1,0:T(8,128)S(1)} %get-tuple-element.49, pred[10]{0:T(512)(128)(4,1)S(1)} %iota_compare_fusion.5, pred[10]{0:T(512)(128)(4,1)S(1)} %iota_compare_fusion.6), kind=kLoop, calls=%fused_computation.2 | loop fusion | flops 1536000 | bytes 3379220 | tf_op jit(solution)/shard_map/add | solution.py:71
  155.0 5.9 %fusion.111 = (f32[10,1,10,6,7,8]{5,4,3,2,1,0:T(8,128)}, f32[10,1,10,6,7,8]{5,4,3,2,1,0:T(8,128)}) fusion(f32[10,10,10,6,8,8]{5,4,3,2,1,0:T(8,128)} %select_add_fusion.2), kind=kLoop, calls=%fused_computation.183 | loop fusion | bytes 537600 | tf_op jit(solution)/shard_map/slice | solution.py:67
  161.0 6.9 %fusion.112 = (f32[10,1,10,6,8,8]{5,4,3,2,1,0:T(8,128)}, f32[10,10,6,8,8]{4,3,2,1,0:T(8,128)}, f32[10,10,6,8,8]{4,3,2,1,0:T(8,128)}, f32[10,1,10,6,8,8]{5,4,3,2,1,0:T(8,128)}) fusion(f32[10,1,10,6,7,8]{5,4,3,2,1,0:T(8,128)} %get-tuple-element.33, f32[10,1,10,6,7,8]{5,4,3,2,1,0:T(8,128)} %get-tuple-element.34), kind=kLoop, calls=%fused_computation.184 | loop fusion | bytes 883200 | tf_op jit(solution)/shard_map/concatenate | solution.py:66
  167.9 14.5 %select_add_fusion.1 = f32[10,10,10,6,8,8]{5,4,3,2,1,0:T(8,128)} fusion(f32[10,10,6,8,8]{4,3,2,1,0:T(8,128)} %get-tuple-element.54, f32[10,10,6,8,8]{4,3,2,1,0:T(8,128)} %get-tuple-element.39, pred[10]{0:T(512)(128)(4,1)S(1)} %iota_compare_fusion.5, pred[10]{0:T(512)(128)(4,1)S(1)} %iota_compare_fusion.6, f32[10,10,6,8,8]{4,3,2,1,0:T(8,128)S(1)} %get-tuple-element.51, ...), kind=kLoop, calls=%fused_computation.1 | loop fusion | flops 3072000 | bytes 3686420 | tf_op jit(solution)/shard_map/add | solution.py:71
  182.4 3.3 fusion.110
  185.7 3.0 fusion.114
  188.7 2.7 fusion.115
  191.5 17.4 %select_add_fusion = f32[10,10,10,6,8,8]{5,4,3,2,1,0:T(8,128)} fusion(f32[10,10,6,8,8]{4,3,2,1,0:T(8,128)} %get-tuple-element.45, f32[10,10,6,8,8]{4,3,2,1,0:T(8,128)} %get-tuple-element.43, pred[10]{0:T(512)(128)(4,1)S(1)} %iota_compare_fusion.5, pred[10]{0:T(512)(128)(4,1)S(1)} %iota_compare_fusion.6, f32[10,10,6,8,8]{4,3,2,1,0:T(8,128)} %get-tuple-element.54, ...), kind=kLoop, calls=%fused_computation | loop fusion | flops 4608000 | bytes 3993620 | tf_op jit(solution)/shard_map/add | solution.py:71
  210.2 2.5 slice_reduce_fusion.11
  215.3 4.5 %slice_reduce_fusion.1 = (f32[10,10,6,8]{3,2,1,0:T(8,128)S(1)}, f32[10,10,6,8]{3,2,1,0:T(8,128)S(1)}) fusion(f32[10,10,10,6,8,8]{5,4,3,2,1,0:T(8,128)} %select_add_fusion), kind=kLoop, calls=%fused_computation.42 | loop fusion | bytes 76800 | tf_op jit(solution)/shard_map/slice | solution.py:96
  219.8 2.2 fusion.109
  222.0 5.0 %slice_reduce_fusion.3 = (f32[10,10,6,8]{3,2,1,0:T(8,128)}, f32[10,10,6,8]{3,2,1,0:T(8,128)}) fusion(f32[10,10,10,6,8,8]{5,4,3,2,1,0:T(8,128)} %select_add_fusion), kind=kLoop, calls=%fused_computation.134 | loop fusion | bytes 76800 | tf_op jit(solution)/shard_map/slice | solution.py:96
  228.3 3.6 broadcast_in_dim.442
  231.9 3.4 broadcast_in_dim.452
  237.2 3.9 broadcast_in_dim.460
  243.1 9.9 %collective-permute-start = (f32[1]{0:T(128)}, f32[1]{0:T(128)}, u32[]{:S(2)}, u32[]{:S(2)}) collective-permute-start(f32[1]{0:T(128)} %bitcast.38), channel_id=1, source_target_pairs={{0,21},{1,22},{2,23},{3,24},{4,25},{5,26},{6,27},{7,28},{8,29},{9,... | collective-permute-start | bytes 20 | tf_op jit(solution)/shard_map/ppermute | solution.py:17
  256.9 6.9 %collective-permute-start.8 = (f32[1]{0:T(128)}, f32[1]{0:T(128)}, u32[]{:S(2)}, u32[]{:S(2)}) collective-permute-start(f32[1]{0:T(128)} %bitcast.47), channel_id=1, source_target_pairs={{0,11},{1,12},{2,13},{3,14},{4,15},{5,16},{6,17},{7,18},{8,19},{9,... | collective-permute-start | bytes 20 | tf_op jit(solution)/shard_map/ppermute | solution.py:17
  277.5 6.4 %collective-permute-start.6 = (f32[1]{0:T(128)}, f32[1]{0:T(128)}, u32[]{:S(2)}, u32[]{:S(2)}) collective-permute-start(f32[1]{0:T(128)} %bitcast.44), channel_id=1, source_target_pairs={{0,13},{1,14},{2,15},{3,16},{4,17},{5,18},{6,19},{7,20},{8,21},{9,... | collective-permute-start | bytes 20 | tf_op jit(solution)/shard_map/ppermute | solution.py:17
  284.5 3.0 collective-permute-start.2
  290.7 3.6 collective-permute-start.14
  297.5 4.5 %collective-permute-start.9 = (f32[60]{0:T(128)S(1)}, f32[60]{0:T(128)S(1)}, u32[]{:S(2)}, u32[]{:S(2)}) collective-permute-start(f32[60]{0:T(128)S(1)} %reshape.230), channel_id=1, source_target_pairs={{0,5},{1,6},{2,7},{3,8},{4,9},{5,10},{6,11},{7,12},{8,13},{9,14},{... | collective-permute-start | bytes 728 | tf_op jit(solution)/shard_map/ppermute | solution.py:17
  307.6 7.9 %collective-permute-start.3 = (f32[80]{0:T(128)S(1)}, f32[80]{0:T(128)S(1)}, u32[]{:S(2)}, u32[]{:S(2)}) collective-permute-start(f32[80]{0:T(128)S(1)} %reshape.224), channel_id=1, source_target_pairs={{0,17},{1,18},{2,19},{3,20},{4,21},{5,22},{6,23},{7,24},{8,25},{9,... | collective-permute-start | bytes 968 | tf_op jit(solution)/shard_map/ppermute | solution.py:17
  323.3 6.7 %collective-permute-start.1 = (f32[80]{0:T(128)S(1)}, f32[80]{0:T(128)S(1)}, u32[]{:S(2)}, u32[]{:S(2)}) collective-permute-start(f32[80]{0:T(128)S(1)} %reshape.222), channel_id=1, source_target_pairs={{0,20},{1,21},{2,22},{3,23},{4,24},{5,25},{6,26},{7,27},{8,28},{9,... | collective-permute-start | bytes 968 | tf_op jit(solution)/shard_map/ppermute | solution.py:17
  331.9 5.4 %collective-permute-start.12 = (f32[4800]{0:T(1024)S(1)}, f32[4800]{0:T(1024)S(1)}, u32[]{:S(2)}, u32[]{:S(2)}) collective-permute-start(f32[4800]{0:T(1024)S(1)} %reshape.233), channel_id=1, source_target_pairs={{0,1},{1,2},{2,3},{3,4},{4,5},{5,6},{6,7},{7,8},{8,9},{9,10},{10,1... | collective-permute-start | bytes 57608 | tf_op jit(solution)/shard_map/ppermute | solution.py:17
  339.4 4.3 %collective-permute-start.10 = (f32[4800]{0:T(1024)S(1)}, f32[4800]{0:T(1024)S(1)}, u32[]{:S(2)}, u32[]{:S(2)}) collective-permute-start(f32[4800]{0:T(1024)S(1)} %reshape.231), channel_id=1, source_target_pairs={{0,4},{1,5},{2,6},{3,7},{4,8},{5,9},{6,10},{7,11},{8,12},{9,13},{1... | collective-permute-start | bytes 57608 | tf_op jit(solution)/shard_map/ppermute | solution.py:17
  352.1 5.6 %collective-permute-start.4 = (f32[6400]{0:T(1024)}, f32[6400]{0:T(1024)}, u32[]{:S(2)}, u32[]{:S(2)}) collective-permute-start(f32[6400]{0:T(1024)} %reshape.225), channel_id=1, source_target_pairs={{0,16},{1,17},{2,18},{3,19},{4,20},{5,21},{6,22},{7,23},{8,24},{9,... | collective-permute-start | bytes 76808 | tf_op jit(solution)/shard_map/ppermute | solution.py:17
  376.0 3.8 broadcast_in_dim.484
  380.0 13.5 %fusion.46 = f32[10,10,10,1,384]{4,2,1,0,3:T(8,128)S(1)} fusion(f32[10,10,10,384]{3,2,1,0:T(8,128)S(1)} %copy-done.3, f32[]{:T(128)} %bitcast.60, f32[10,384]{1,0:T(8,128)S(1)} %copy-done.18, f32[]{:T(128)} %bitcast.57, f32[10,384]{1,0:T(8,128)S(1)} %copy-done.22, f32[10,10,384]{2,1,0:T(8,128)} %broadcast_in_dim.546, f32[10,384]{1,0:T(8,128)S(1)} %copy-done.23, ...), kind=kOutput, calls=%fused_computation.67 | convolution fusion | flops 1811859456 | bytes 5103412 | tf_op jit(solution)/shard_map/abcj,ij->abci/dot_general | solution.py:190
  393.5 2.7 copy.48
  (252 shorter events, 84.0 us)
Async XLA Ops:
  11.6 31.0 %all-to-all-start.2 = ((f32[5,10,10,2,384]{4,2,1,0,3:T(8,128)}), f32[5,10,10,2,384]{4,2,1,0,3:T(8,128)S(1)}, u32[]{:S(2)}, u32[]{:S(2)}) async-start(f32[5,10,10,2,384]{4,2,1,0,3:T(8,128)} %copy.45), calls=%async_computation.2 | async-start | bytes 4915200 | tf_op jit(solution)/shard_map/all_to_all | solution.py:159
  18.9 29.9 %copy-start.31 = (s32[1,384]{1,0:T(1,128)S(1)}, s32[1,384]{1,0:T(1,128)}, u32[]{:S(2)}) copy-start(s32[1,384]{1,0:T(1,128)} %param.6) | copy-start | bytes 4612
  42.6 32.4 %all-to-all-start.1 = ((f32[5,10,10,2,384]{4,2,1,0,3:T(8,128)}), f32[5,10,10,2,384]{4,2,1,0,3:T(8,128)}, u32[]{:S(2)}, u32[]{:S(2)}) async-start(f32[5,10,10,2,384]{4,2,1,0,3:T(8,128)} %copy.42), calls=%async_computation.1 | async-start | bytes 4915200 | tf_op jit(solution)/shard_map/all_to_all | solution.py:158
  48.8 55.7 %copy-start.29 = (s32[384]{0:T(512)}, s32[384]{0:T(512)S(1)}, u32[]{:S(2)}) copy-start(s32[384]{0:T(512)S(1)} %reduce) | copy-start | bytes 4612
  53.0 138.5 %copy-start.25 = (pred[10]{0:T(512)(128)(4,1)}, pred[10]{0:T(512)(128)(4,1)S(1)}, u32[]{:S(2)}) copy-start(pred[10]{0:T(512)(128)(4,1)S(1)} %iota_compare_fusion.6) | copy-start | bytes 34
  75.0 21.7 %all-to-all-start = ((f32[2,5,10,10,1,384]{5,4,3,2,1,0:T(1,128)}), f32[2,5,10,10,1,384]{5,4,3,2,1,0:T(1,128)}, u32[]{:S(2)}, u32[]{:S(2)}) async-start(f32[2,5,10,10,1,384]{5,4,3,2,1,0:T(1,128)} %pad_maximum_fusion), calls=%async_computation | async-start | bytes 3072000 | tf_op jit(solution)/shard_map/all_to_all | solution.py:153
  81.2 110.3 %copy-start.27 = (pred[10]{0:T(512)(128)(4,1)}, pred[10]{0:T(512)(128)(4,1)S(1)}, u32[]{:S(2)}) copy-start(pred[10]{0:T(512)(128)(4,1)S(1)} %iota_compare_fusion.5) | copy-start | bytes 34
  90.8 7.5 %copy-start.7 = (f32[10,10,384,10]{2,3,1,0:T(8,128)S(1)}, f32[10,10,384,10]{2,3,1,0:T(8,128)}, u32[]{:S(2)}) copy-start(f32[10,10,384,10]{2,3,1,0:T(8,128)} %fusion.120) | copy-start | bytes 4608004
  107.4 15.4 %copy-start.2 = (f32[10,10,10,384]{3,2,1,0:T(8,128)}, f32[10,10,10,384]{3,2,1,0:T(8,128)S(1)}, u32[]{:S(2)}) copy-start(f32[10,10,10,384]{3,2,1,0:T(8,128)S(1)} %fusion.23) | copy-start | bytes 4608004
  134.1 33.8 %slice-start = ((s8[24576000]{0:T(1024)(128)(4,1)}), s8[4194304]{0:T(1024)(128)(4,1)S(1)}, s32[]{:S(2)}) async-start(s8[24576000]{0:T(1024)(128)(4,1)} %bitcast.192), calls=%async_computation.3 | async-start | bytes 8388608
  134.1 33.8 %slice-start.1 = ((s8[24576000]{0:T(1024)(128)(4,1)}), s8[4194304]{0:T(1024)(128)(4,1)S(1)}, s32[]{:S(2)}) async-start(s8[24576000]{0:T(1024)(128)(4,1)} %bitcast.192), calls=%async_computation.4 | async-start | bytes 8388608
  134.1 33.8 %slice-start.2 = ((s8[24576000]{0:T(1024)(128)(4,1)}), s8[4194304]{0:T(1024)(128)(4,1)S(1)}, s32[]{:S(2)}) async-start(s8[24576000]{0:T(1024)(128)(4,1)} %bitcast.192), calls=%async_computation.5 | async-start | bytes 8388608
  134.1 33.8 %slice-start.3 = ((s8[24576000]{0:T(1024)(128)(4,1)}), s8[4194304]{0:T(1024)(128)(4,1)S(1)}, s32[]{:S(2)}) async-start(s8[24576000]{0:T(1024)(128)(4,1)} %bitcast.192), calls=%async_computation.6 | async-start | bytes 8388608
  134.1 33.8 %slice-start.4 = ((s8[24576000]{0:T(1024)(128)(4,1)}), s8[4194304]{0:T(1024)(128)(4,1)S(1)}, s32[]{:S(2)}) async-start(s8[24576000]{0:T(1024)(128)(4,1)} %bitcast.192), calls=%async_computation.7 | async-start | bytes 8388608
  161.0 6.9 %slice-start.5 = ((s8[24576000]{0:T(1024)(128)(4,1)}), s8[3604480]{0:T(1024)(128)(4,1)S(1)}, s32[]{:S(2)}) async-start(s8[24576000]{0:T(1024)(128)(4,1)} %bitcast.192), calls=%async_computation.8 | async-start | bytes 7208960
  219.8 7.3 %copy-start.6 = (f32[1,10,10,6,8,8]{5,4,3,0,2,1:T(8,128)S(1)}, f32[1,10,10,6,8,8]{5,4,3,0,2,1:T(8,128)}, u32[]{:S(2)}) copy-start(f32[1,10,10,6,8,8]{5,4,3,0,2,1:T(8,128)} %get-tuple-element.50) | copy-start | bytes 460804
  228.3 7.0 %copy-start.4 = (f32[10,1,10,6,8,8]{5,4,3,2,1,0:T(8,128)S(1)}, f32[10,1,10,6,8,8]{5,4,3,2,1,0:T(8,128)}, u32[]{:S(2)}) copy-start(f32[10,1,10,6,8,8]{5,4,3,2,1,0:T(8,128)} %get-tuple-element.55) | copy-start | bytes 460804
  243.1 31.7 %copy-start.9 = (f32[1,10,10,1,8,8]{5,4,3,2,1,0:T(8,128)S(1)}, f32[1,10,10,1,8,8]{5,4,3,2,1,0:T(8,128)}, u32[]{:S(2)}) copy-start(f32[1,10,10,1,8,8]{5,4,3,2,1,0:T(8,128)} %get-tuple-element.30) | copy-start | bytes 76804
  243.1 32.5 %collective-permute-start = (f32[1]{0:T(128)}, f32[1]{0:T(128)}, u32[]{:S(2)}, u32[]{:S(2)}) collective-permute-start(f32[1]{0:T(128)} %bitcast.38), channel_id=1, source_target_pairs={{0,21},{1,22},{2,23},{3,24},{4,25},{5,26},{6,27},{7,28},{8,29},{9,... | collective-permute-start | bytes 20 | tf_op jit(solution)/shard_map/ppermute | solution.py:17
  253.0 24.5 %collective-permute-start.25 = (f32[1]{0:T(128)}, f32[1]{0:T(128)}, u32[]{:S(2)}, u32[]{:S(2)}) collective-permute-start(f32[1]{0:T(128)} %bitcast.59), channel_id=1, source_target_pairs={{21,0},{22,1},{23,2},{24,3},{25,4},{26,5},{27,6},{28,7},{29,8},{30... | collective-permute-start | bytes 20 | tf_op jit(solution)/shard_map/ppermute | solution.py:17
  254.3 30.2 %collective-permute-start.19 = (f32[1]{0:T(128)}, f32[1]{0:T(128)}, u32[]{:S(2)}, u32[]{:S(2)}) collective-permute-start(f32[1]{0:T(128)} %bitcast.53), channel_id=1, source_target_pairs={{13,0},{14,1},{15,2},{16,3},{17,4},{18,5},{19,6},{20,7},{21,8},{22... | collective-permute-start | bytes 20 | tf_op jit(solution)/shard_map/ppermute | solution.py:17
  255.6 32.5 %collective-permute-start.17 = (f32[1]{0:T(128)}, f32[1]{0:T(128)}, u32[]{:S(2)}, u32[]{:S(2)}) collective-permute-start(f32[1]{0:T(128)} %bitcast.50), channel_id=1, source_target_pairs={{11,0},{12,1},{13,2},{14,3},{15,4},{16,5},{17,6},{18,7},{19,8},{20... | collective-permute-start | bytes 20 | tf_op jit(solution)/shard_map/ppermute | solution.py:17
  256.9 33.8 %collective-permute-start.8 = (f32[1]{0:T(128)}, f32[1]{0:T(128)}, u32[]{:S(2)}, u32[]{:S(2)}) collective-permute-start(f32[1]{0:T(128)} %bitcast.47), channel_id=1, source_target_pairs={{0,11},{1,12},{2,13},{3,14},{4,15},{5,16},{6,17},{7,18},{8,19},{9,... | collective-permute-start | bytes 20 | tf_op jit(solution)/shard_map/ppermute | solution.py:17
  275.6 19.4 %collective-permute-start.23 = (f32[1]{0:T(128)}, f32[1]{0:T(128)}, u32[]{:S(2)}, u32[]{:S(2)}) collective-permute-start(f32[1]{0:T(128)} %bitcast.56), channel_id=1, source_target_pairs={{19,0},{20,1},{21,2},{22,3},{23,4},{24,5},{25,6},{26,7},{27,8},{28... | collective-permute-start | bytes 20 | tf_op jit(solution)/shard_map/ppermute | solution.py:17
  277.5 20.0 %collective-permute-start.6 = (f32[1]{0:T(128)}, f32[1]{0:T(128)}, u32[]{:S(2)}, u32[]{:S(2)}) collective-permute-start(f32[1]{0:T(128)} %bitcast.44), channel_id=1, source_target_pairs={{0,13},{1,14},{2,15},{3,16},{4,17},{5,18},{6,19},{7,20},{8,21},{9,... | collective-permute-start | bytes 20 | tf_op jit(solution)/shard_map/ppermute | solution.py:17
  284.5 18.1 %collective-permute-start.2 = (f32[1]{0:T(128)}, f32[1]{0:T(128)}, u32[]{:S(2)}, u32[]{:S(2)}) collective-permute-start(f32[1]{0:T(128)} %bitcast.41), channel_id=1, source_target_pairs={{0,19},{1,20},{2,21},{3,22},{4,23},{5,24},{6,25},{7,26},{8,27},{9,... | collective-permute-start | bytes 20 | tf_op jit(solution)/shard_map/ppermute | solution.py:17
  288.1 16.8 %collective-permute-start.11 = (f32[60]{0:T(128)S(1)}, f32[60]{0:T(128)S(1)}, u32[]{:S(2)}, u32[]{:S(2)}) collective-permute-start(f32[60]{0:T(128)S(1)} %reshape.232), channel_id=1, source_target_pairs={{0,3},{1,4},{2,5},{3,6},{4,7},{5,8},{6,9},{7,10},{8,11},{9,12},{10... | collective-permute-start | bytes 728 | tf_op jit(solution)/shard_map/ppermute | solution.py:17
  290.7 15.6 %collective-permute-start.14 = (f32[60]{0:T(128)S(1)}, f32[60]{0:T(128)S(1)}, u32[]{:S(2)}, u32[]{:S(2)}) collective-permute-start(f32[60]{0:T(128)S(1)} %reshape.235), channel_id=1, source_target_pairs={{3,0},{4,1},{5,2},{6,3},{7,4},{8,5},{9,6},{10,7},{11,8},{12,9},{13... | collective-permute-start | bytes 728 | tf_op jit(solution)/shard_map/ppermute | solution.py:17
  295.0 12.6 %collective-permute-start.16 = (f32[60]{0:T(128)S(1)}, f32[60]{0:T(128)S(1)}, u32[]{:S(2)}, u32[]{:S(2)}) collective-permute-start(f32[60]{0:T(128)S(1)} %reshape.237), channel_id=1, source_target_pairs={{5,0},{6,1},{7,2},{8,3},{9,4},{10,5},{11,6},{12,7},{13,8},{14,9},{... | collective-permute-start | bytes 728 | tf_op jit(solution)/shard_map/ppermute | solution.py:17
  297.5 18.2 %collective-permute-start.9 = (f32[60]{0:T(128)S(1)}, f32[60]{0:T(128)S(1)}, u32[]{:S(2)}, u32[]{:S(2)}) collective-permute-start(f32[60]{0:T(128)S(1)} %reshape.230), channel_id=1, source_target_pairs={{0,5},{1,6},{2,7},{3,8},{4,9},{5,10},{6,11},{7,12},{8,13},{9,14},{... | collective-permute-start | bytes 728 | tf_op jit(solution)/shard_map/ppermute | solution.py:17
  302.6 18.0 %collective-permute-start.5 = (f32[80]{0:T(128)S(1)}, f32[80]{0:T(128)S(1)}, u32[]{:S(2)}, u32[]{:S(2)}) collective-permute-start(f32[80]{0:T(128)S(1)} %reshape.226), channel_id=1, source_target_pairs={{0,15},{1,16},{2,17},{3,18},{4,19},{5,20},{6,21},{7,22},{8,23},{9,... | collective-permute-start | bytes 968 | tf_op jit(solution)/shard_map/ppermute | solution.py:17
  304.9 17.0 %collective-permute-start.20 = (f32[80]{0:T(128)S(1)}, f32[80]{0:T(128)S(1)}, u32[]{:S(2)}, u32[]{:S(2)}) collective-permute-start(f32[80]{0:T(128)S(1)} %reshape.241), channel_id=1, source_target_pairs={{15,0},{16,1},{17,2},{18,3},{19,4},{20,5},{21,6},{22,7},{23,8},{24... | collective-permute-start | bytes 968 | tf_op jit(solution)/shard_map/ppermute | solution.py:17
  306.3 17.0 %collective-permute-start.22 = (f32[80]{0:T(128)S(1)}, f32[80]{0:T(128)S(1)}, u32[]{:S(2)}, u32[]{:S(2)}) collective-permute-start(f32[80]{0:T(128)S(1)} %reshape.243), channel_id=1, source_target_pairs={{17,0},{18,1},{19,2},{20,3},{21,4},{22,5},{23,6},{24,7},{25,8},{26... | collective-permute-start | bytes 968 | tf_op jit(solution)/shard_map/ppermute | solution.py:17
  307.6 22.4 %collective-permute-start.3 = (f32[80]{0:T(128)S(1)}, f32[80]{0:T(128)S(1)}, u32[]{:S(2)}, u32[]{:S(2)}) collective-permute-start(f32[80]{0:T(128)S(1)} %reshape.224), channel_id=1, source_target_pairs={{0,17},{1,18},{2,19},{3,20},{4,21},{5,22},{6,23},{7,24},{8,25},{9,... | collective-permute-start | bytes 968 | tf_op jit(solution)/shard_map/ppermute | solution.py:17
  315.7 16.2 %collective-permute-start.7 = (f32[80]{0:T(128)S(1)}, f32[80]{0:T(128)S(1)}, u32[]{:S(2)}, u32[]{:S(2)}) collective-permute-start(f32[80]{0:T(128)S(1)} %reshape.228), channel_id=1, source_target_pairs={{0,12},{1,13},{2,14},{3,15},{4,16},{5,17},{6,18},{7,19},{8,20},{9,... | collective-permute-start | bytes 968 | tf_op jit(solution)/shard_map/ppermute | solution.py:17
  320.6 16.8 %collective-permute-start.18 = (f32[80]{0:T(128)S(1)}, f32[80]{0:T(128)S(1)}, u32[]{:S(2)}, u32[]{:S(2)}) collective-permute-start(f32[80]{0:T(128)S(1)} %reshape.239), channel_id=1, source_target_pairs={{12,0},{13,1},{14,2},{15,3},{16,4},{17,5},{18,6},{19,7},{20,8},{21... | collective-permute-start | bytes 968 | tf_op jit(solution)/shard_map/ppermute | solution.py:17
  322.0 17.4 %collective-permute-start.24 = (f32[80]{0:T(128)S(1)}, f32[80]{0:T(128)S(1)}, u32[]{:S(2)}, u32[]{:S(2)}) collective-permute-start(f32[80]{0:T(128)S(1)} %reshape.245), channel_id=1, source_target_pairs={{20,0},{21,1},{22,2},{23,3},{24,4},{25,5},{26,6},{27,7},{28,8},{29... | collective-permute-start | bytes 968 | tf_op jit(solution)/shard_map/ppermute | solution.py:17
  323.3 20.4 %collective-permute-start.1 = (f32[80]{0:T(128)S(1)}, f32[80]{0:T(128)S(1)}, u32[]{:S(2)}, u32[]{:S(2)}) collective-permute-start(f32[80]{0:T(128)S(1)} %reshape.222), channel_id=1, source_target_pairs={{0,20},{1,21},{2,22},{3,23},{4,24},{5,25},{6,26},{7,27},{8,28},{9,... | collective-permute-start | bytes 968 | tf_op jit(solution)/shard_map/ppermute | solution.py:17
  330.0 22.1 %collective-permute-start.13 = (f32[4800]{0:T(1024)S(1)}, f32[4800]{0:T(1024)S(1)}, u32[]{:S(2)}, u32[]{:S(2)}) collective-permute-start(f32[4800]{0:T(1024)S(1)} %reshape.234), channel_id=1, source_target_pairs={{1,0},{2,1},{3,2},{4,3},{5,4},{6,5},{7,6},{8,7},{9,8},{10,9},{11,1... | collective-permute-start | bytes 57608 | tf_op jit(solution)/shard_map/ppermute | solution.py:17
  331.9 25.8 %collective-permute-start.12 = (f32[4800]{0:T(1024)S(1)}, f32[4800]{0:T(1024)S(1)}, u32[]{:S(2)}, u32[]{:S(2)}) collective-permute-start(f32[4800]{0:T(1024)S(1)} %reshape.233), channel_id=1, source_target_pairs={{0,1},{1,2},{2,3},{3,4},{4,5},{5,6},{6,7},{7,8},{8,9},{9,10},{10,1... | collective-permute-start | bytes 57608 | tf_op jit(solution)/shard_map/ppermute | solution.py:17
  337.4 20.4 %collective-permute-start.15 = (f32[4800]{0:T(1024)S(1)}, f32[4800]{0:T(1024)S(1)}, u32[]{:S(2)}, u32[]{:S(2)}) collective-permute-start(f32[4800]{0:T(1024)S(1)} %reshape.236), channel_id=1, source_target_pairs={{4,0},{5,1},{6,2},{7,3},{8,4},{9,5},{10,6},{11,7},{12,8},{13,9},{1... | collective-permute-start | bytes 57608 | tf_op jit(solution)/shard_map/ppermute | solution.py:17
  339.4 18.4 %collective-permute-start.10 = (f32[4800]{0:T(1024)S(1)}, f32[4800]{0:T(1024)S(1)}, u32[]{:S(2)}, u32[]{:S(2)}) collective-permute-start(f32[4800]{0:T(1024)S(1)} %reshape.231), channel_id=1, source_target_pairs={{0,4},{1,5},{2,6},{3,7},{4,8},{5,9},{6,10},{7,11},{8,12},{9,13},{1... | collective-permute-start | bytes 57608 | tf_op jit(solution)/shard_map/ppermute | solution.py:17
  343.7 28.2 %collective-permute-start.21 = (f32[6400]{0:T(1024)}, f32[6400]{0:T(1024)S(1)}, u32[]{:S(2)}, u32[]{:S(2)}) collective-permute-start(f32[6400]{0:T(1024)} %reshape.242), channel_id=1, source_target_pairs={{16,0},{17,1},{18,2},{19,3},{20,4},{21,5},{22,6},{23,7},{24,8},{25... | collective-permute-start | bytes 76808 | tf_op jit(solution)/shard_map/ppermute | solution.py:17
  352.1 19.5 %collective-permute-start.4 = (f32[6400]{0:T(1024)}, f32[6400]{0:T(1024)}, u32[]{:S(2)}, u32[]{:S(2)}) collective-permute-start(f32[6400]{0:T(1024)} %reshape.225), channel_id=1, source_target_pairs={{0,16},{1,17},{2,18},{3,19},{4,20},{5,21},{6,22},{7,23},{8,24},{9,... | collective-permute-start | bytes 76808 | tf_op jit(solution)/shard_map/ppermute | solution.py:17
  374.2 5.6 %copy-start.15 = (f32[10,384]{1,0:T(8,128)S(1)}, f32[10,384]{1,0:T(8,128)}, u32[]{:S(2)}) copy-start(f32[10,384]{1,0:T(8,128)} %broadcast_in_dim.522) | copy-start | bytes 46084
  374.2 5.6 %copy-start.16 = (f32[10,384]{1,0:T(8,128)S(1)}, f32[10,384]{1,0:T(8,128)}, u32[]{:S(2)}) copy-start(f32[10,384]{1,0:T(8,128)} %broadcast_in_dim.510) | copy-start | bytes 46084
  374.3 5.6 %copy-start.17 = (f32[10,384]{1,0:T(8,128)S(1)}, f32[10,384]{1,0:T(8,128)}, u32[]{:S(2)}) copy-start(f32[10,384]{1,0:T(8,128)} %broadcast_in_dim.473) | copy-start | bytes 46084
  374.3 5.6 %copy-start.18 = (f32[10,384]{1,0:T(8,128)S(1)}, f32[10,384]{1,0:T(8,128)}, u32[]{:S(2)}) copy-start(f32[10,384]{1,0:T(8,128)} %broadcast_in_dim.556) | copy-start | bytes 46084
  (27 other events, 114.1 us)
